TPU v7x, 32 devices: a whole 2x2x4 slice. The times are simulated.
32 devices in a mesh: groups: 2 (over y), ep: 4 (over z), dp: 4 (over x, core), tp: 1.
Axes of the slice: x: 2, y: 2, z: 4, core: 2. Of those that a mesh axis runs over, the one named last changes fastest.
Arguments:
- tokens: bfloat16 [2048, 2048], P(('groups', 'ep', 'dp', 'tp')), parts along dimension 0, may hold values from -6 to 6
- experts_one: int32 [2048, 8], P(('groups', 'ep', 'dp', 'tp')), parts along dimension 0, may hold values from 0 to 15, all different within a row; in each aligned block of 64 rows (0 to 63, 64 to 127, ...) at most 40 rows name the same one
- gates_one: float32 [2048, 8], P(('groups', 'ep', 'dp', 'tp')), parts along dimension 0, may hold values from 0.05 to 0.5
- w_in_one: bfloat16 [16, 2048, 2, 768], P(('ep', 'dp'), None, None, 'tp'), may hold values from -0.125 to 0.125
- w_down_one: bfloat16 [16, 768, 2048], P(('ep', 'dp'), 'tp'), may hold values from -0.21875 to 0.21875
- norm_gain: float32 [2048], replicated, may hold values from 0.5 to 1.5
- experts_two: int32 [2048, 8], P(('groups', 'ep', 'dp', 'tp')), parts along dimension 0, may hold values from 0 to 15, all different within a row; in each aligned block of 64 rows (0 to 63, 64 to 127, ...) at most 40 rows name the same one
- gates_two: float32 [2048, 8], P(('groups', 'ep', 'dp', 'tp')), parts along dimension 0, may hold values from 0.05 to 0.5
- placement_two: int32 [16], replicated, may hold values from 0 to 15, each once
- w_in_two: bfloat16 [16, 2048, 2, 768], P(('ep', 'dp'), None, None, 'tp'), may hold values from -0.125 to 0.125
- w_down_two: bfloat16 [16, 768, 2048], P(('ep', 'dp'), 'tp'), may hold values from -0.21875 to 0.21875
Outputs:
- layer_out: bfloat16 [2048, 2048], P(('groups', 'ep', 'dp', 'tp')), parts along dimension 0
There are 2 independent parts, one for each index of `groups`. A program takes and returns all parts, laid end to end along the dimension named above; an argument that names none is the same for every part. Nothing has to cross between parts.
Inputs may be any that keep to these rules, and one draw needn't show every extreme that they name: `experts_one`: each token names 8 different experts; among the 64 tokens of one device no expert is named more than 40 times, and on some device some expert is named exactly 40 times. `experts_two`: each token names 8 different experts; among the 64 tokens of one device no expert is named more than 40 times, and on some device some expert is named exactly 40 times. `placement_two`: each slot is named by exactly one expert.
All inputs are finite; a program needn't handle non-finite values.
Results may differ from a plain program's by a relative error of at most 0.011.
Values may be sent and summed in bfloat16 or wider, within the bound.
A program may use at most 128 MiB of HBM per device.

v0:
```python
import jax
import jax.numpy as jnp
from jax import lax
from jax.sharding import PartitionSpec as P


def capacity(tok_rows, top_count, expert_count):
    return max(2, min(tok_rows, 5 * tok_rows * top_count // (4 * expert_count)))


def pack_rows(rows_in, targets, expert_count, per_slot):
    tok_rows, top_count = targets.shape
    flat_ids = targets.reshape(-1)
    hit_table = (flat_ids[:, None] == jnp.arange(expert_count, dtype=jnp.int32)[None, :]).astype(
        jnp.int32
    )
    before = jnp.cumsum(hit_table, axis=0) - hit_table
    slot_rank = jnp.sum(before * hit_table, axis=1)
    slot_index = flat_ids * per_slot + slot_rank
    source = jnp.arange(tok_rows * top_count, dtype=jnp.int32) // top_count
    owner_row = jnp.zeros((expert_count * per_slot,), jnp.int32).at[slot_index].set(source)
    filled = jnp.zeros((expert_count * per_slot,), jnp.int32).at[slot_index].set(1)
    buffer = jnp.where(filled[:, None] > 0, rows_in[owner_row], jnp.zeros((), rows_in.dtype))
    return (buffer, slot_index)


def to_experts(buffer, expert_count, per_slot):
    row_width = buffer.shape[1]
    arrived = lax.all_to_all(
        buffer.reshape(expert_count, per_slot, row_width),
        ("ep", "dp"),
        split_axis=0,
        concat_axis=0,
        tiled=True,
    )
    return arrived.reshape(expert_count * per_slot, row_width)


def to_owners(produced, expert_count, per_slot):
    row_width = produced.shape[1]
    returned = lax.all_to_all(
        produced.reshape(expert_count, per_slot, row_width),
        ("ep", "dp"),
        split_axis=0,
        concat_axis=0,
        tiled=True,
    )
    return returned.reshape(expert_count * per_slot, row_width)


def run_expert(received, w_in, w_down):
    row_width = received.shape[1]
    down_local = w_down[0]
    half_width = down_local.shape[0]
    w_local = w_in.reshape(row_width, 2 * half_width)
    gate_up = jnp.dot(
        lax.all_gather(received, "tp", axis=0, tiled=True),
        w_local,
        preferred_element_type=jnp.float32,
    )
    hidden = (jax.nn.silu(gate_up[:, :half_width]) * gate_up[:, half_width:]).astype(jnp.bfloat16)
    return lax.psum_scatter(
        jnp.dot(hidden, down_local, preferred_element_type=jnp.float32).astype(jnp.bfloat16),
        "tp",
        scatter_dimension=0,
        tiled=True,
    )


def moe_block(rows_in, targets, gate_values, w_in, w_down, expert_count, per_slot):
    tok_rows, top_count = targets.shape
    row_width = rows_in.shape[1]
    buffer, slot_index = pack_rows(rows_in, targets, expert_count, per_slot)
    arrived = to_experts(buffer, expert_count, per_slot)
    produced = run_expert(arrived, w_in, w_down)
    returned = to_owners(produced, expert_count, per_slot)
    picked = returned[slot_index].reshape(tok_rows, top_count, row_width)
    return jnp.sum(gate_values[:, :, None] * picked.astype(jnp.float32), axis=1)


def shards(
    tokens,
    experts_one,
    gates_one,
    w_in_one,
    w_down_one,
    norm_gain,
    experts_two,
    gates_two,
    placement_two,
    w_in_two,
    w_down_two,
):
    tok_rows, top_count = experts_one.shape
    expert_count = placement_two.shape[0]
    per_slot = capacity(tok_rows, top_count, expert_count)
    moe_one = moe_block(
        tokens, experts_one, gates_one, w_in_one, w_down_one, expert_count, per_slot
    )
    mixed = (tokens.astype(jnp.float32) + moe_one).astype(jnp.bfloat16)
    mixed = lax.optimization_barrier(mixed)
    mixed_wide = mixed.astype(jnp.float32)
    inv_rms = lax.rsqrt(jnp.mean(mixed_wide * mixed_wide, axis=1, keepdims=True) + 1e-06)
    normed = (mixed_wide * inv_rms * norm_gain[None, :]).astype(jnp.bfloat16)
    expert_range = jnp.arange(expert_count, dtype=jnp.int32)
    matches = experts_two[:, :, None] == expert_range[None, None, :]
    layer_slots = jnp.sum(jnp.where(matches, placement_two[None, None, :], 0), axis=2)
    moe_two = moe_block(
        normed, layer_slots, gates_two, w_in_two, w_down_two, expert_count, per_slot
    )
    return (mixed_wide + moe_two).astype(jnp.bfloat16)


def solution(mesh):
    in_specs = (
        P(("groups", "ep", "dp", "tp"), None),
        P(("groups", "ep", "dp", "tp"), None),
        P(("groups", "ep", "dp", "tp"), None),
        P(("ep", "dp"), None, None, "tp"),
        P(("ep", "dp"), "tp", None),
        P(),
        P(("groups", "ep", "dp", "tp"), None),
        P(("groups", "ep", "dp", "tp"), None),
        P(),
        P(("ep", "dp"), None, None, "tp"),
        P(("ep", "dp"), "tp", None),
    )
    out_specs = P(("groups", "ep", "dp", "tp"), None)
    return jax.shard_map(shards, mesh=mesh, in_specs=in_specs, out_specs=out_specs, check_vma=False)
```

profile of v0, /device:TPU:11, one launch (start us, length us, event | category | flops | bytes accessed | tf_op | source)
XLA Modules:
  0.0 317.4 jit_solution(6289434253920874725)
XLA Ops:
  0.0 0.0 copy-start
  0.0 0.9 copy.28
  0.9 0.1 eq.67
  1.0 0.1 eq.63
  1.1 0.7 broadcast_multiply_fusion.1
  1.8 1.2 reduce-window.14
  3.0 0.2 slice_reduce_fusion.1
  3.2 0.1 copy.27
  3.3 0.1 mul.82
  3.4 0.1 fusion.19
  3.5 2.4 scatter_custom_fusion.1
  6.0 2.4 scatter_custom_fusion
  8.5 0.1 broadcast_in_dim.57
  8.6 0.0 copy-done.2
  8.6 4.1 %gather_fusion = bf16[640,2048]{1,0:T(8,128)(2,1)} fusion(bf16[64,2048]{1,0:T(8,128)(2,1)S(1)} %copy-done.2, s32[1024]{0:T(1024)S(1)} %pad_clamp_fusion.3), kind=kCustom, calls=%fused_computation | custom fusion | bytes 5245440 | tf_op jit(solution)/shard_map/gather | solution.py:23
  12.7 3.5 %broadcast_select_fusion.1 = bf16[16,40,2048]{2,1,0:T(8,128)(2,1)} fusion(bf16[16,40,2048]{2,1,0:T(8,128)(2,1)} %bitcast.74, pred[16,40]{1,0:T(8,128)(4,1)S(1)} %broadcast_in_dim.57), kind=kLoop, calls=%fused_computation.17 | loop fusion | flops 1310720 | bytes 5243520 | tf_op jit(solution)/shard_map/jit(_where)/select_n | solution.py:23
  16.2 6.5 %all-to-all-start = ((bf16[16,40,2048]{2,1,0:T(8,128)(2,1)}), bf16[16,40,2048]{2,1,0:T(8,128)(2,1)}, u32[]{:S(2)}, u32[]{:S(2)}) async-start(bf16[16,40,2048]{2,1,0:T(8,128)(2,1)} %broadcast_select_fusion.1), calls=%async_computation | async-start | bytes 5242880 | tf_op jit(solution)/shard_map/all_to_all | solution.py:29
  22.7 6.8 %copy.38 = bf16[256,8,2,768]{3,1,2,0:T(8,128)(2,1)} copy(bf16[256,8,2,768]{3,2,1,0:T(2,128)(2,1)} %bitcast.75) | data formatting | bytes 12582912
  29.5 52.0 %all-to-all-done = bf16[16,40,2048]{2,1,0:T(8,128)(2,1)} async-done(((bf16[16,40,2048]{2,1,0:T(8,128)(2,1)}), bf16[16,40,2048]{2,1,0:T(8,128)(2,1)}, u32[]{:S(2)}, u32[]{:S(2)}) %all-to-all-start) | async-done | bytes 2621472 | tf_op jit(solution)/shard_map/all_to_all | solution.py:29
  81.5 7.1 %fusion.35 = f32[640,1536]{1,0:T(8,128)S(1)} fusion(bf16[640,2048]{1,0:T(8,128)(2,1)} %bitcast.4, bf16[2048,1536]{1,0:T(8,128)(2,1)} %bitcast.77), kind=kOutput, calls=%fused_computation.82 | convolution fusion | flops 4026531840 | bytes 12845056 | tf_op jit(solution)/shard_map/dot_general | solution.py:56
  88.6 0.0 copy-done
  88.6 3.8 %convolution_convert_fusion.1 = bf16[640,2048]{1,0:T(8,128)(2,1)} fusion(bf16[1,768,2048]{2,1,0:T(8,128)(2,1)S(1)} %copy-done, f32[640,1536]{1,0:T(8,128)S(1)} %fusion.35), kind=kOutput, calls=%fused_computation.13 | convolution fusion | flops 2017525760 | bytes 9699328 | tf_op jit(solution)/shard_map/dot_general | solution.py:63
  92.4 4.9 %all-to-all-start.1 = ((bf16[16,40,2048]{2,1,0:T(8,128)(2,1)}), bf16[16,40,2048]{2,1,0:T(8,128)(2,1)S(1)}, u32[]{:S(2)}, u32[]{:S(2)}) async-start(bf16[16,40,2048]{2,1,0:T(8,128)(2,1)} %bitcast.79), calls=%async_computation.1 | async-start | bytes 5242880 | tf_op jit(solution)/shard_map/all_to_all | solution.py:41
  97.3 0.0 copy-done.8
  97.3 0.0 copy-done.9
  97.3 0.1 select_reduce_fusion
  97.4 0.1 copy.33
  97.5 0.1 eq.78
  97.6 0.1 eq.74
  97.7 1.2 reduce-window.16
  98.8 0.2 slice_reduce_fusion
  99.1 0.1 copy.32
  99.2 0.1 mul.89
  99.3 0.1 fusion.16
  99.4 2.4 scatter_custom_fusion.3
  101.8 2.6 scatter_custom_fusion.2
  104.5 0.0 copy-done.6
  104.5 0.1 copy.26
  104.6 0.1 broadcast_in_dim.63
  104.7 51.2 %all-to-all-done.1 = bf16[16,40,2048]{2,1,0:T(8,128)(2,1)S(1)} async-done(((bf16[16,40,2048]{2,1,0:T(8,128)(2,1)}), bf16[16,40,2048]{2,1,0:T(8,128)(2,1)S(1)}, u32[]{:S(2)}, u32[]{:S(2)}) %all-to-all-start.1) | async-done | bytes 2621472 | tf_op jit(solution)/shard_map/all_to_all | solution.py:41
  155.9 3.3 %gather_fusion.1 = bf16[512,2048]{1,0:T(8,128)(2,1)} fusion(bf16[640,2048]{1,0:T(8,128)(2,1)S(1)} %bitcast.72, s32[1024]{0:T(1024)S(1)} %pad_clamp_fusion.2), kind=kCustom, calls=%fused_computation.1 | custom fusion | bytes 4196352 | tf_op jit(solution)/shard_map/gather | solution.py:77
  159.3 3.4 %fusion.1 = f32[64,2048]{1,0:T(8,128)S(1)} fusion(bf16[512,2048]{1,0:T(8,128)(2,1)} %gather_fusion.1, f32[64,8]{1,0:T(8,128)S(1)} %copy.26), kind=kLoop, calls=%fused_computation.11 | loop fusion | flops 3014656 | bytes 2623488 | tf_op jit(solution)/shard_map/reduce_sum | solution.py:78
  162.8 0.0 copy-start.3
  162.8 0.2 fusion.10
  162.9 0.0 copy-done.5
  162.9 0.1 fusion.12
  163.1 3.4 %gather_fusion.2 = bf16[640,2048]{1,0:T(8,128)(2,1)S(1)} fusion(bf16[64,2048]{1,0:T(8,128)(2,1)S(1)} %fusion.12, s32[1024]{0:T(1024)S(1)} %pad_clamp_fusion.1), kind=kCustom, calls=%fused_computation.2 | custom fusion | bytes 5245440 | tf_op jit(solution)/shard_map/gather | solution.py:23
  166.5 0.0 copy-done.3
  166.5 1.8 broadcast_select_fusion
  168.3 4.8 %all-to-all-start.2 = ((bf16[16,40,2048]{2,1,0:T(8,128)(2,1)}), bf16[16,40,2048]{2,1,0:T(8,128)(2,1)S(1)}, u32[]{:S(2)}, u32[]{:S(2)}) async-start(bf16[16,40,2048]{2,1,0:T(8,128)(2,1)} %broadcast_select_fusion), calls=%async_computation.2 | async-start | bytes 5242880 | tf_op jit(solution)/shard_map/all_to_all | solution.py:29
  173.1 6.8 %copy.39 = bf16[256,8,2,768]{3,1,2,0:T(8,128)(2,1)} copy(bf16[256,8,2,768]{3,2,1,0:T(2,128)(2,1)} %bitcast.76) | data formatting | bytes 12582912
  179.9 51.9 %all-to-all-done.2 = bf16[16,40,2048]{2,1,0:T(8,128)(2,1)S(1)} async-done(((bf16[16,40,2048]{2,1,0:T(8,128)(2,1)}), bf16[16,40,2048]{2,1,0:T(8,128)(2,1)S(1)}, u32[]{:S(2)}, u32[]{:S(2)}) %all-to-all-start.2) | async-done | bytes 2621472 | tf_op jit(solution)/shard_map/all_to_all | solution.py:29
  231.8 6.5 %fusion.36 = f32[640,1536]{1,0:T(8,128)S(1)} fusion(bf16[640,2048]{1,0:T(8,128)(2,1)S(1)} %bitcast.80, bf16[2048,1536]{1,0:T(8,128)(2,1)} %bitcast.78), kind=kOutput, calls=%fused_computation.83 | convolution fusion | flops 4026531840 | bytes 12845056 | tf_op jit(solution)/shard_map/dot_general | solution.py:56
  238.2 0.0 copy-done.10
  238.2 3.8 %convolution_convert_fusion = bf16[640,2048]{1,0:T(8,128)(2,1)} fusion(bf16[1,768,2048]{2,1,0:T(8,128)(2,1)S(1)} %copy-done.10, f32[640,1536]{1,0:T(8,128)S(1)} %fusion.36), kind=kOutput, calls=%fused_computation.12 | convolution fusion | flops 2017525760 | bytes 9699328 | tf_op jit(solution)/shard_map/dot_general | solution.py:63
  242.0 4.9 %all-to-all-start.3 = ((bf16[16,40,2048]{2,1,0:T(8,128)(2,1)}), bf16[16,40,2048]{2,1,0:T(8,128)(2,1)}, u32[]{:S(2)}, u32[]{:S(2)}) async-start(bf16[16,40,2048]{2,1,0:T(8,128)(2,1)} %bitcast.15), calls=%async_computation.3 | async-start | bytes 5242880 | tf_op jit(solution)/shard_map/all_to_all | solution.py:41
  246.9 0.0 copy-done.7
  246.9 0.1 copy.31
  247.0 58.7 %all-to-all-done.3 = bf16[16,40,2048]{2,1,0:T(8,128)(2,1)} async-done(((bf16[16,40,2048]{2,1,0:T(8,128)(2,1)}), bf16[16,40,2048]{2,1,0:T(8,128)(2,1)}, u32[]{:S(2)}, u32[]{:S(2)}) %all-to-all-start.3) | async-done | bytes 2621472 | tf_op jit(solution)/shard_map/all_to_all | solution.py:41
  305.7 7.4 %gather_fusion.3 = bf16[512,2048]{1,0:T(8,128)(2,1)} fusion(bf16[640,2048]{1,0:T(8,128)(2,1)} %bitcast.16, s32[1024]{0:T(1024)S(1)} %pad_clamp_fusion), kind=kCustom, calls=%fused_computation.3 | custom fusion | bytes 4196352 | tf_op jit(solution)/shard_map/gather | solution.py:77
  313.1 3.5 %fusion = f32[64,2048]{1,0:T(8,128)S(1)} fusion(bf16[512,2048]{1,0:T(8,128)(2,1)} %gather_fusion.3, f32[64,8]{1,0:T(8,128)S(1)} %copy.31), kind=kLoop, calls=%fused_computation.9 | loop fusion | flops 3014656 | bytes 2623488 | tf_op jit(solution)/shard_map/reduce_sum | solution.py:78
  316.6 0.0 copy-done.4
  316.6 0.8 fusion.13
  317.4 0.0 copy-done.1
  (30 shorter events, 0.2 us)
Async XLA Ops:
  0.0 88.6 %copy-start = (bf16[1,768,2048]{2,1,0:T(8,128)(2,1)S(1)}, bf16[1,768,2048]{2,1,0:T(8,128)(2,1)}, u32[]{:S(2)}) copy-start(bf16[1,768,2048]{2,1,0:T(8,128)(2,1)} %param.15) | copy-start | bytes 9437188
  0.0 8.6 %copy-start.2 = (bf16[64,2048]{1,0:T(8,128)(2,1)S(1)}, bf16[64,2048]{1,0:T(8,128)(2,1)}, u32[]{:S(2)}) copy-start(bf16[64,2048]{1,0:T(8,128)(2,1)} %param.11) | copy-start | bytes 786436
  16.2 65.3 %all-to-all-start = ((bf16[16,40,2048]{2,1,0:T(8,128)(2,1)}), bf16[16,40,2048]{2,1,0:T(8,128)(2,1)}, u32[]{:S(2)}, u32[]{:S(2)}) async-start(bf16[16,40,2048]{2,1,0:T(8,128)(2,1)} %broadcast_select_fusion.1), calls=%async_computation | async-start | bytes 5242880 | tf_op jit(solution)/shard_map/all_to_all | solution.py:29
  92.4 4.9 %copy-start.8 = (s32[64,8]{0,1:T(8,128)S(1)}, s32[64,8]{0,1:T(8,128)}, u32[]{:S(2)}) copy-start(s32[64,8]{0,1:T(8,128)} %param.17) | copy-start | bytes 6148
  92.4 4.9 %copy-start.9 = (s32[16]{0:T(128)S(1)}, s32[16]{0:T(128)}, u32[]{:S(2)}) copy-start(s32[16]{0:T(128)} %param.19) | copy-start | bytes 196
  92.4 12.1 %copy-start.6 = (f32[64,8]{0,1:T(8,128)S(1)}, f32[64,8]{0,1:T(8,128)}, u32[]{:S(2)}) copy-start(f32[64,8]{0,1:T(8,128)} %param.13) | copy-start | bytes 6148
  92.4 63.6 %all-to-all-start.1 = ((bf16[16,40,2048]{2,1,0:T(8,128)(2,1)}), bf16[16,40,2048]{2,1,0:T(8,128)(2,1)S(1)}, u32[]{:S(2)}, u32[]{:S(2)}) async-start(bf16[16,40,2048]{2,1,0:T(8,128)(2,1)} %bitcast.79), calls=%async_computation.1 | async-start | bytes 5242880 | tf_op jit(solution)/shard_map/all_to_all | solution.py:41
  159.3 3.7 %copy-start.5 = (f32[2048]{0:T(1024)S(1)}, f32[2048]{0:T(1024)}, u32[]{:S(2)}) copy-start(f32[2048]{0:T(1024)} %param.16) | copy-start | bytes 24580
  162.8 3.8 %copy-start.3 = (bf16[64,2048]{1,0:T(8,128)(2,1)}, bf16[64,2048]{1,0:T(8,128)(2,1)S(1)}, u32[]{:S(2)}) copy-start(bf16[64,2048]{1,0:T(8,128)(2,1)S(1)} %add_convert_fusion) | copy-start | bytes 786436
  168.3 63.4 %all-to-all-start.2 = ((bf16[16,40,2048]{2,1,0:T(8,128)(2,1)}), bf16[16,40,2048]{2,1,0:T(8,128)(2,1)S(1)}, u32[]{:S(2)}, u32[]{:S(2)}) async-start(bf16[16,40,2048]{2,1,0:T(8,128)(2,1)} %broadcast_select_fusion), calls=%async_computation.2 | async-start | bytes 5242880 | tf_op jit(solution)/shard_map/all_to_all | solution.py:29
  231.8 6.5 %copy-start.10 = (bf16[1,768,2048]{2,1,0:T(8,128)(2,1)S(1)}, bf16[1,768,2048]{2,1,0:T(8,128)(2,1)}, u32[]{:S(2)}) copy-start(bf16[1,768,2048]{2,1,0:T(8,128)(2,1)} %param.21) | copy-start | bytes 9437188
  242.0 4.9 %copy-start.7 = (f32[64,8]{0,1:T(8,128)S(1)}, f32[64,8]{0,1:T(8,128)}, u32[]{:S(2)}) copy-start(f32[64,8]{0,1:T(8,128)} %param.18) | copy-start | bytes 6148
  242.0 63.7 %all-to-all-start.3 = ((bf16[16,40,2048]{2,1,0:T(8,128)(2,1)}), bf16[16,40,2048]{2,1,0:T(8,128)(2,1)}, u32[]{:S(2)}, u32[]{:S(2)}) async-start(bf16[16,40,2048]{2,1,0:T(8,128)(2,1)} %bitcast.15), calls=%async_computation.3 | async-start | bytes 5242880 | tf_op jit(solution)/shard_map/all_to_all | solution.py:41
  305.7 11.7 %copy-start.1 = (bf16[1,768,2048]{2,1,0:T(8,128)(2,1)S(1)}, bf16[1,768,2048]{2,1,0:T(8,128)(2,1)}, u32[]{:S(2)}) copy-start(bf16[1,768,2048]{2,1,0:T(8,128)(2,1)} %param.15) | copy-start | bytes 9437188
  313.1 3.5 %copy-start.4 = (bf16[64,2048]{1,0:T(8,128)(2,1)S(1)}, bf16[64,2048]{1,0:T(8,128)(2,1)}, u32[]{:S(2)}) copy-start(bf16[64,2048]{1,0:T(8,128)(2,1)} %copy-done.3) | copy-start | bytes 786436
where the time goes:
time: 318 us; the launch traced here: 317 us
  waiting for transfers between devices  214 us (67%)
  local copies, waits for them, and re-layouts  44.4 us (14%)
  starting transfers between devices  21.1 us (7%)
  matrix products  21.1 us (7%)
  other arithmetic  16.7 us (5%)
    all_to_all x2, waiting for transfers between devices, to_owners(): lax.all_to_all(produced.reshape(expert_count, per_slot, row_width), ('ep'...  110 us
    all_to_all x2, waiting for transfers between devices, to_experts(): lax.all_to_all(buffer.reshape(expert_count, per_slot, row_width), ('ep',...  104 us
    unnamed x27, local copies, waits for them, and re-layouts  14.7 us
    dot_general x2, matrix products, run_expert(): jnp.dot(lax.all_gather(received, 'tp', axis=0, tiled=True), w_local, pref...  13.6 us
    all_to_all x2, starting transfers between devices, to_experts(): lax.all_to_all(buffer.reshape(expert_count, per_slot, row_width), ('ep',...  11.3 us
    gather x2, local copies, waits for them, and re-layouts, moe_block(): picked = returned[slot_index].reshape(tok_rows, top_count, row_width)  10.8 us
    all_to_all x2, starting transfers between devices, to_owners(): lax.all_to_all(produced.reshape(expert_count, per_slot, row_width), ('ep'...  9.81 us
    dot_general x2, matrix products, run_expert(): jnp.dot(hidden, down_local, preferred_element_type=jnp.float32)  7.54 us
  transfers between devices with their start and end apart: 4, of which 4 were waited for; matrix products, arithmetic and copies ran while one was open for 7% of the time, Pallas kernels for 0%

commit v1 on v0

v1 whole, which is shorter than its diff:
```python
import jax
import jax.numpy as jnp
from jax import lax
from jax.sharding import PartitionSpec as P

ALL = ("ep", "dp", "tp")


def expert_weight(targets, gate_values, expert_id):
    return jnp.sum(jnp.where(targets == expert_id, gate_values, 0.0), axis=1)


def moe_dense(rows_in, targets, gate_values, w_in, w_down):
    row_width = rows_in.shape[1]
    half_width = w_down.shape[1]
    my_expert = lax.axis_index("ep") * lax.axis_size("dp") + lax.axis_index("dp")
    rows = lax.all_gather(rows_in, ALL, axis=0, tiled=True)
    targets = lax.all_gather(targets, ALL, axis=0, tiled=True)
    gate_values = lax.all_gather(gate_values, ALL, axis=0, tiled=True)
    weight = expert_weight(targets, gate_values, my_expert)
    gate_up = jnp.dot(rows, w_in.reshape(row_width, 2 * half_width), preferred_element_type=jnp.float32)
    hidden = (jax.nn.silu(gate_up[:, :half_width]) * gate_up[:, half_width:]).astype(jnp.bfloat16)
    out = jnp.dot(hidden, w_down[0], preferred_element_type=jnp.float32)
    out = (out * weight[:, None]).astype(jnp.bfloat16)
    return lax.psum_scatter(out, ALL, scatter_dimension=0, tiled=True).astype(jnp.float32)


def shards(tokens, experts_one, gates_one, w_in_one, w_down_one, norm_gain, experts_two, gates_two, placement_two, w_in_two, w_down_two):
    moe_one = moe_dense(tokens, experts_one, gates_one, w_in_one, w_down_one)
    mixed = (tokens.astype(jnp.float32) + moe_one).astype(jnp.bfloat16)
    mixed_wide = mixed.astype(jnp.float32)
    inv_rms = lax.rsqrt(jnp.mean(mixed_wide * mixed_wide, axis=1, keepdims=True) + 1e-06)
    normed = (mixed_wide * inv_rms * norm_gain[None, :]).astype(jnp.bfloat16)
    expert_range = jnp.arange(placement_two.shape[0], dtype=jnp.int32)
    matches = experts_two[:, :, None] == expert_range[None, None, :]
    layer_slots = jnp.sum(jnp.where(matches, placement_two[None, None, :], 0), axis=2)
    moe_two = moe_dense(normed, layer_slots, gates_two, w_in_two, w_down_two)
    return (mixed_wide + moe_two).astype(jnp.bfloat16)


def solution(mesh):
    rows = P(("groups", "ep", "dp", "tp"), None)
    w_in = P(("ep", "dp"), None, None, "tp")
    w_down = P(("ep", "dp"), "tp", None)
    in_specs = (rows, rows, rows, w_in, w_down, P(), rows, rows, P(), w_in, w_down)
    return jax.shard_map(shards, mesh=mesh, in_specs=in_specs, out_specs=rows, check_vma=False)
```

time: 318 us -> 298 us (0.937)
  the two profiles are of different devices: /device:TPU:11 before, /device:TPU:0 now
where the time goes in v1:
time: 298 us
  waiting for transfers between devices  156 us (52%)
  blocking collectives  80 us (27%)
  matrix products  30.3 us (10%)
  local copies, waits for them, and re-layouts  13.8 us (5%)
  between operations  13.2 us (4%)
  other arithmetic  4.87 us (2%)
    reduce_scatter x2, waiting for transfers between devices, moe_dense(): lax.psum_scatter(out, ALL, scatter_dimension=0, tiled=True)  143 us
    all_gather x2, blocking collectives, moe_dense(): targets = lax.all_gather(targets, ALL, axis=0, tiled=True)  43.2 us
    all_gather x2, blocking collectives, moe_dense(): gate_values = lax.all_gather(gate_values, ALL, axis=0, tiled=True)  36.8 us
    dot_general x2, matrix products, moe_dense(): jnp.dot(rows, w_in.reshape(row_width, 2 * half_width), preferred_element_...  20.1 us
    unnamed x16, local copies, waits for them, and re-layouts  13.7 us
    all_gather x2, waiting for transfers between devices, moe_dense(): rows = lax.all_gather(rows_in, ALL, axis=0, tiled=True)  11.7 us
    dot_general x2, matrix products, moe_dense(): out = jnp.dot(hidden, w_down[0], preferred_element_type=jnp.float32)  10.2 us
  transfers between devices with their start and end apart: 4, of which 4 were waited for; matrix products, arithmetic and copies ran while one was open for 5% of the time, Pallas kernels for 0%

profile of v1, /device:TPU:0, one launch (start us, length us, event | category | flops | bytes accessed | tf_op | source)
XLA Modules:
  0.0 297.9 jit_solution(11222166767860984814)
XLA Ops:
  6.5 0.0 copy-start
  6.5 0.0 all-gather.7.cloned.1.call-start
  6.5 0.7 all-gather.7.cloned.1.call-update
  7.3 0.0 reduce-scatter.3.cloned.1.call-start
  7.3 23.9 %all-gather = s32[16,64,8]{1,2,0:T(8,128)S(1)} all-gather(s32[1,64,8]{1,2,0:T(8,128)} %bitcast.25), channel_id=1, replica_groups=mesh['groups'=2,'ep'=4,'dp'=4,'tp'=1] {'ep','dp','tp'}, dimensions={0}, use_global_device_ids=true | all-gather | bytes 34816 | tf_op jit(solution)/shard_map/all_gather | solution.py:18
  31.2 18.3 %all-gather.1 = f32[16,64,8]{1,2,0:T(8,128)S(1)} all-gather(f32[1,64,8]{1,2,0:T(8,128)} %bitcast.26), channel_id=1, replica_groups=mesh['groups'=2,'ep'=4,'dp'=4,'tp'=1] {'ep','dp','tp'}, dimensions={0}, use_global_device_ids=true | all-gather | bytes 34816 | tf_op jit(solution)/shard_map/all_gather | solution.py:19
  49.5 0.1 reshape.37
  49.5 6.8 %copy.14 = bf16[256,8,2,768]{3,1,2,0:T(8,128)(2,1)} copy(bf16[256,8,2,768]{3,2,1,0:T(2,128)(2,1)} %bitcast.20) | data formatting | bytes 12582912
  56.4 6.6 %all-gather.7.cloned.1.call-done = bf16[1024,2048]{1,0:T(8,128)(2,1)} async-done(((bf16[64,2048]{1,0:T(8,128)(2,1)}), bf16[1024,2048]{1,0:T(8,128)(2,1)}) %all-gather.7.cloned.1.call-update) | async-done | bytes 4194320 | tf_op jit(solution)/shard_map/all_gather | solution.py:17
  63.0 10.0 %fusion.14 = f32[1024,1536]{1,0:T(8,128)S(1)} fusion(bf16[1024,2048]{1,0:T(8,128)(2,1)} %all-gather.7.cloned.1.call-done, bf16[2048,1536]{1,0:T(8,128)(2,1)} %bitcast.23), kind=kOutput, calls=%fused_computation.25 | convolution fusion | flops 6442450944 | bytes 16777216 | tf_op jit(solution)/shard_map/dot_general | solution.py:21
  73.0 0.0 copy-done
  73.0 5.1 %multiply_convert_fusion.1 = bf16[1024,2048]{1,0:T(8,128)(2,1)} fusion(f32[1024]{0:T(1024)S(1)} %reshape.37, bf16[1,768,2048]{2,1,0:T(8,128)(2,1)S(1)} %copy-done, f32[1024,1536]{1,0:T(8,128)S(1)} %fusion.14), kind=kOutput, calls=%fused_computation.1 | convolution fusion | flops 3230138368 | bytes 13635584 | tf_op jit(solution)/shard_map/dot_general | solution.py:23
  78.0 0.0 copy-start.1
  78.0 0.0 copy-start.2
  78.0 0.0 reduce-scatter.3.cloned.1.call-update
  78.1 0.0 all-gather.9.cloned.1.call-start
  78.1 71.5 %reduce-scatter.3.cloned.1.call-done = bf16[64,2048]{1,0:T(8,128)(2,1)} async-done(((bf16[1024,2048]{1,0:T(8,128)(2,1)}), bf16[64,2048]{1,0:T(8,128)(2,1)}) %reduce-scatter.3.cloned.1.call-update) | async-done | bytes 262160 | tf_op jit(solution)/shard_map/reduce_scatter | solution.py:25
  149.6 0.0 copy-done.1
  149.6 1.1 fusion.8
  150.8 0.0 copy-done.2
  150.8 1.8 fusion.10
  152.6 0.0 all-gather.9.cloned.1.call-update
  152.6 0.0 reduce-scatter.5.cloned.1.call-start
  152.6 0.0 copy-start.4
  152.6 0.0 copy-start.5
  152.7 0.0 copy-start.3
  152.7 6.8 %copy.15 = bf16[256,8,2,768]{3,1,2,0:T(8,128)(2,1)} copy(bf16[256,8,2,768]{3,2,1,0:T(2,128)(2,1)} %bitcast.21) | data formatting | bytes 12582912
  159.5 0.0 copy-done.4
  159.5 0.0 copy-done.5
  159.5 0.1 select_reduce_fusion.2
  159.6 19.4 %all-gather.2 = s32[16,64,8]{1,2,0:T(8,128)S(1)} all-gather(s32[1,64,8]{1,2,0:T(8,128)S(1)} %bitcast.24), channel_id=1, replica_groups=mesh['groups'=2,'ep'=4,'dp'=4,'tp'=1] {'ep','dp','tp'}, dimensions={0}, use_global_device_ids=true | all-gather | bytes 34816 | tf_op jit(solution)/shard_map/all_gather | solution.py:18
  178.9 0.0 copy-done.3
  178.9 18.5 %all-gather.3 = f32[16,64,8]{1,2,0:T(8,128)S(1)} all-gather(f32[1,64,8]{1,2,0:T(8,128)S(1)} %bitcast.27), channel_id=1, replica_groups=mesh['groups'=2,'ep'=4,'dp'=4,'tp'=1] {'ep','dp','tp'}, dimensions={0}, use_global_device_ids=true | all-gather | bytes 34816 | tf_op jit(solution)/shard_map/all_gather | solution.py:19
  197.5 0.1 reshape.38
  197.6 5.1 %all-gather.9.cloned.1.call-done = bf16[1024,2048]{1,0:T(8,128)(2,1)} async-done(((bf16[64,2048]{1,0:T(8,128)(2,1)}), bf16[1024,2048]{1,0:T(8,128)(2,1)}) %all-gather.9.cloned.1.call-update) | async-done | bytes 4194320 | tf_op jit(solution)/shard_map/all_gather | solution.py:17
  202.7 0.0 copy-start.6
  202.7 10.1 %fusion.15 = f32[1024,1536]{1,0:T(8,128)S(1)} fusion(bf16[1024,2048]{1,0:T(8,128)(2,1)} %all-gather.9.cloned.1.call-done, bf16[2048,1536]{1,0:T(8,128)(2,1)} %bitcast.22), kind=kOutput, calls=%fused_computation.26 | convolution fusion | flops 6442450944 | bytes 16777216 | tf_op jit(solution)/shard_map/dot_general | solution.py:21
  212.8 0.0 copy-done.6
  212.8 5.1 %multiply_convert_fusion = bf16[1024,2048]{1,0:T(8,128)(2,1)} fusion(f32[1024]{0:T(1024)S(1)} %reshape.38, bf16[1,768,2048]{2,1,0:T(8,128)(2,1)S(1)} %copy-done.6, f32[1024,1536]{1,0:T(8,128)S(1)} %fusion.15), kind=kOutput, calls=%fused_computation | convolution fusion | flops 3230138368 | bytes 13635584 | tf_op jit(solution)/shard_map/dot_general | solution.py:23
  217.9 0.0 reduce-scatter.5.cloned.1.call-update
  218.0 71.6 %reduce-scatter.5.cloned.1.call-done = bf16[64,2048]{1,0:T(8,128)(2,1)} async-done(((bf16[1024,2048]{1,0:T(8,128)(2,1)}), bf16[64,2048]{1,0:T(8,128)(2,1)}) %reduce-scatter.5.cloned.1.call-update) | async-done | bytes 262160 | tf_op jit(solution)/shard_map/reduce_scatter | solution.py:25
  289.6 1.8 fusion.11
  (3 shorter events, 0.1 us)
Async XLA Ops:
  6.5 66.4 %copy-start = (bf16[1,768,2048]{2,1,0:T(8,128)(2,1)S(1)}, bf16[1,768,2048]{2,1,0:T(8,128)(2,1)}, u32[]{:S(2)}) copy-start(bf16[1,768,2048]{2,1,0:T(8,128)(2,1)} %param.15) | copy-start | bytes 9437188
  6.5 56.4 %all-gather.7.cloned.1.call-start = ((), (), s32[]{:S(2)}) async-start(), calls=%async_computation.2 | async-start | bytes 4456448 | tf_op jit(solution)/shard_map/all_gather | solution.py:17
  7.3 142.4 %reduce-scatter.3.cloned.1.call-start = ((), (), s32[]{:S(2)}) async-start(), calls=%async_computation.3 | async-start | bytes 4456448 | tf_op jit(solution)/shard_map/reduce_scatter | solution.py:25
  78.0 71.6 %copy-start.1 = (bf16[64,2048]{1,0:T(8,128)(2,1)S(1)}, bf16[64,2048]{1,0:T(8,128)(2,1)}, u32[]{:S(2)}) copy-start(bf16[64,2048]{1,0:T(8,128)(2,1)} %param.11) | copy-start | bytes 786436
  78.0 72.7 %copy-start.2 = (f32[2048]{0:T(1024)S(1)}, f32[2048]{0:T(1024)}, u32[]{:S(2)}) copy-start(f32[2048]{0:T(1024)} %param.16) | copy-start | bytes 24580
  78.1 124.6 %all-gather.9.cloned.1.call-start = ((), (), s32[]{:S(2)}) async-start(), calls=%async_computation.4 | async-start | bytes 4456448 | tf_op jit(solution)/shard_map/all_gather | solution.py:17
  152.6 137.0 %reduce-scatter.5.cloned.1.call-start = ((), (), s32[]{:S(2)}) async-start(), calls=%async_computation.5 | async-start | bytes 4456448 | tf_op jit(solution)/shard_map/reduce_scatter | solution.py:25
  152.6 6.8 %copy-start.4 = (s32[64,8]{0,1:T(8,128)S(1)}, s32[64,8]{0,1:T(8,128)}, u32[]{:S(2)}) copy-start(s32[64,8]{0,1:T(8,128)} %param.17) | copy-start | bytes 6148
  152.6 6.8 %copy-start.5 = (s32[16]{0:T(128)S(1)}, s32[16]{0:T(128)}, u32[]{:S(2)}) copy-start(s32[16]{0:T(128)} %param.19) | copy-start | bytes 196
  152.7 26.3 %copy-start.3 = (f32[64,8]{0,1:T(8,128)S(1)}, f32[64,8]{0,1:T(8,128)}, u32[]{:S(2)}) copy-start(f32[64,8]{0,1:T(8,128)} %param.18) | copy-start | bytes 6148
  202.7 10.2 %copy-start.6 = (bf16[1,768,2048]{2,1,0:T(8,128)(2,1)S(1)}, bf16[1,768,2048]{2,1,0:T(8,128)(2,1)}, u32[]{:S(2)}) copy-start(bf16[1,768,2048]{2,1,0:T(8,128)(2,1)} %param.21) | copy-start | bytes 9437188
Sparse Core Ops, SparseCore 0:
  9.5 53.4 all-gather.6
  78.2 71.3 reduce-scatter.2
  152.7 49.9 all-gather.8
  218.1 71.4 reduce-scatter.4

commit v2 on v0

--- a/solution.py
+++ b/solution.py
@@ -1,7 +1,190 @@
+import functools
+
 import jax
 import jax.numpy as jnp
 from jax import lax
+from jax.experimental import pallas as pl
+from jax.experimental.pallas import tpu as pltpu
 from jax.sharding import PartitionSpec as P
+
+MESH = pl.DeviceIdType.MESH
+LANES = 128
+
+
+def layer_kernel(
+    n, experts, width, blk, w_in_hbm, w_down_hbm, out,
+    rows, part, core_in, cross, x_in, line, z_in, w_in, w_down, hidden,
+    w_sem, z_send, z_recv, x_send, x_recv, c_send, c_recv, d_send, d_recv,
+    rc_send, rc_recv, rx_send, rx_recv, rz_send, rz_recv,
+):
+    z = lax.axis_index("ep")
+    d = lax.axis_index("dp")
+    mine = z * lax.axis_size("dp") + d
+    x_peer = {"dp": (d + 2) % 4}
+    c_peer = {"dp": d + 1 - 2 * (d % 2)}
+    half = w_down.shape[0]
+    tok = blk.shape[0]
+    order = sorted(range(n), key=lambda k: (min(k, n - k), k))
+
+    def remote(src, dst, send, recv, to):
+        return pltpu.make_async_remote_copy(
+            src_ref=src, dst_ref=dst, send_sem=send, recv_sem=recv, device_id=to, device_id_type=MESH
+        )
+
+    load_in = pltpu.make_async_copy(w_in_hbm, w_in, w_sem.at[0])
+    load_down = pltpu.make_async_copy(w_down_hbm, w_down, w_sem.at[1])
+    load_in.start()
+    load_down.start()
+
+    barrier = pltpu.get_barrier_semaphore()
+    for k in range(1, n):
+        pl.semaphore_signal(barrier, inc=1, device_id={"ep": (z + k) % n}, device_id_type=MESH)
+    pl.semaphore_signal(barrier, inc=1, device_id=x_peer, device_id_type=MESH)
+    pl.semaphore_signal(barrier, inc=1, device_id=c_peer, device_id_type=MESH)
+    pl.semaphore_wait(barrier, n + 1)
+
+    sends = []
+
+    def go(copy):
+        copy.start()
+        sends.append(copy)
+        return copy
+
+    z_copy = {}
+    for k in order[1:]:
+        z_copy[k] = go(remote(blk, rows.at[k, 0], z_send.at[k], z_recv.at[k], {"ep": (z + n - k) % n}))
+    x_copy, c_copy, d_copy = {}, {}, {}
+
+    def spread(k):
+        src = blk if k == 0 else rows.at[k, 0]
+        x_copy[k] = go(remote(src, rows.at[k, 1], x_send.at[k], x_recv.at[k], x_peer))
+        c_copy[k] = go(remote(src, rows.at[k, 2], c_send.at[k], c_recv.at[k], c_peer))
+
+    spread(0)
+    rows[0, 0] = blk[...]
+    rc_copy, rx_copy, rz_copy = {}, {}, {}
+
+    def finish(k):
+        rx_copy[k].wait_recv()
+        total = (
+            part[k, 0].astype(jnp.float32) + core_in[k, 0].astype(jnp.float32) + x_in[k].astype(jnp.float32)
+        )
+        if k == 0:
+            out[...] = total
+        else:
+            line[k] = total.astype(line.dtype)
+            rz_copy[n - k] = go(
+                remote(line.at[k], z_in.at[n - k], rz_send.at[k], rz_recv.at[n - k], {"ep": (z + k) % n})
+            )
+
+    for i, k in enumerate(order):
+        x_copy[k].wait_recv()
+        d_copy[k] = go(remote(rows.at[k, 1], rows.at[k, 3], d_send.at[k], d_recv.at[k], c_peer))
+        if i + 1 < n:
+            later = order[i + 1]
+            z_copy[later].wait_recv()
+            spread(later)
+        c_copy[k].wait_recv()
+        d_copy[k].wait_recv()
+        if i == 0:
+            load_in.wait()
+            load_down.wait()
+        gates = rows[k, :, :, width:].reshape(4 * tok, LANES).astype(jnp.float32)
+        lane = lax.broadcasted_iota(jnp.int32, (4 * tok, LANES), 1)
+        weight = jnp.sum(jnp.where((lane == mine) | (lane == mine + experts), gates, 0.0), axis=1, keepdims=True)
+        step = 256 if half % 256 == 0 else LANES
+
+        @pl.loop(0, half // step)
+        def _(j):
+            x = rows[k, :, :, :width].reshape(4 * tok, width)
+            at = pl.multiple_of(j * step, step)
+            gate = jnp.dot(x, w_in[:, pl.ds(at, step)], preferred_element_type=jnp.float32)
+            up = jnp.dot(x, w_in[:, pl.ds(half + at, step)], preferred_element_type=jnp.float32)
+            hidden[:, pl.ds(at, step)] = (gate / (1.0 + jnp.exp(-gate)) * up).astype(hidden.dtype)
+
+        wide = 256 if width % 256 == 0 else LANES
+
+        @pl.loop(0, width // wide)
+        def _(j):
+            at = pl.multiple_of(j * wide, wide)
+            y = jnp.dot(hidden[...], w_down[:, pl.ds(at, wide)], preferred_element_type=jnp.float32)
+            y = jnp.where(weight == 0.0, 0.0, y * weight)
+            part[k, :, :, pl.ds(at, wide)] = y.astype(part.dtype).reshape(4, tok, wide)
+
+        rc_copy[k] = go(remote(part.at[k, pl.ds(2, 2)], core_in.at[k], rc_send.at[k], rc_recv.at[k], c_peer))
+        if i > 0:
+            finish(order[i - 1])
+        rc_copy[k].wait_recv()
+        cross[k] = (part[k, 1].astype(jnp.float32) + core_in[k, 1].astype(jnp.float32)).astype(cross.dtype)
+        rx_copy[k] = go(remote(cross.at[k], x_in.at[k], rx_send.at[k], rx_recv.at[k], x_peer))
+    finish(order[-1])
+    for k in order[1:]:
+        rz_copy[k].wait_recv()
+        out[...] += z_in[k].astype(jnp.float32)
+    for copy in sends:
+        copy.wait_send()
+
+
+def expert_layer(block, w_in, w_down, experts, number):
+    tok, wide = block.shape
+    half, width = w_down.shape[1:]
+    n = lax.axis_size("ep")
+    bf16 = jnp.bfloat16
+    dma = pltpu.SemaphoreType.DMA
+    return pl.pallas_call(
+        functools.partial(layer_kernel, n, experts, width),
+        out_shape=jax.ShapeDtypeStruct((tok, width), jnp.float32),
+        in_specs=[
+            pl.BlockSpec(memory_space=pltpu.VMEM),
+            pl.BlockSpec(memory_space=pl.ANY),
+            pl.BlockSpec(memory_space=pl.ANY),
+        ],
+        out_specs=pl.BlockSpec(memory_space=pltpu.VMEM),
+        scratch_shapes=[
+            pltpu.VMEM((n, 4, tok, wide), bf16),
+            pltpu.VMEM((n, 4, tok, width), bf16),
+            pltpu.VMEM((n, 2, tok, width), bf16),
+            pltpu.VMEM((n, tok, width), bf16),
+            pltpu.VMEM((n, tok, width), bf16),
+            pltpu.VMEM((n, tok, width), bf16),
+            pltpu.VMEM((n, tok, width), bf16),
+            pltpu.VMEM((width, 2 * half), bf16),
+            pltpu.VMEM((half, width), bf16),
+            pltpu.VMEM((4 * tok, half), bf16),
+            dma((2,)),
+        ]
+        + [dma((n,))] * 14,
+        compiler_params=pltpu.CompilerParams(
+            collective_id=number, has_side_effects=True, vmem_limit_bytes=56 * 1024 * 1024
+        ),
+        name=f"layer_{number}",
+    )(block, w_in.reshape(width, 2 * half), w_down.reshape(half, width))
+
+
+def with_gates(rows_in, targets, gate_values, experts):
+    matches = targets[:, :, None] == jnp.arange(experts, dtype=jnp.int32)[None, None, :]
+    table = jnp.sum(jnp.where(matches, gate_values[:, :, None], 0.0), axis=1)
+    high = table.astype(jnp.bfloat16)
+    low = (table - high.astype(jnp.float32)).astype(jnp.bfloat16)
+    rest = jnp.zeros((rows_in.shape[0], LANES - 2 * experts), jnp.bfloat16)
+    return jnp.concatenate([rows_in, high, low, rest], axis=1)
+
+
+def fused_shards(
+    tokens, experts_one, gates_one, w_in_one, w_down_one, norm_gain,
+    experts_two, gates_two, placement_two, w_in_two, w_down_two,
+):
+    experts = placement_two.shape[0]
+    expert_range = jnp.arange(experts, dtype=jnp.int32)
+    matches = experts_two[:, :, None] == expert_range[None, None, :]
+    layer_slots = jnp.sum(jnp.where(matches, placement_two[None, None, :], 0), axis=2)
+    moe_one = expert_layer(with_gates(tokens, experts_one, gates_one, experts), w_in_one, w_down_one, experts, 0)
+    mixed = (tokens.astype(jnp.float32) + moe_one).astype(jnp.bfloat16)
+    mixed_wide = mixed.astype(jnp.float32)
+    inv_rms = lax.rsqrt(jnp.mean(mixed_wide * mixed_wide, axis=1, keepdims=True) + 1e-06)
+    normed = (mixed_wide * inv_rms * norm_gain[None, :]).astype(jnp.bfloat16)
+    moe_two = expert_layer(with_gates(normed, layer_slots, gates_two, experts), w_in_two, w_down_two, experts, 1)
+    return (mixed_wide + moe_two).astype(jnp.bfloat16)
 
 
 def capacity(tok_rows, top_count, expert_count):
@@ -126,4 +309,5 @@
         P(("ep", "dp"), "tp", None),
     )
     out_specs = P(("groups", "ep", "dp", "tp"), None)
-    return jax.shard_map(shards, mesh=mesh, in_specs=in_specs, out_specs=out_specs, check_vma=False)
+    fused = mesh.shape["tp"] == 1 and mesh.shape["dp"] == 4 and mesh.shape["ep"] <= 4
+    return jax.shard_map(fused_shards if fused else shards, mesh=mesh, in_specs=in_specs, out_specs=out_specs, check_vma=False)

time: 318 us -> 178 us (0.56)
  the two profiles are of different devices: /device:TPU:11 before, /device:TPU:31 now
where the time goes in v2:
time: 178 us
  Pallas kernels  155 us (87%)
  local copies, waits for them, and re-layouts  16.6 us (9%)
  other arithmetic  5.39 us (3%)
    pallas_call x2, Pallas kernels, expert_layer(): pl.pallas_call(functools.partial(layer_kernel, n, experts, width), out_sh...  155 us
    unnamed x6, local copies, waits for them, and re-layouts  13.6 us

profile of v2, /device:TPU:31, one launch (start us, length us, event | category | flops | bytes accessed | tf_op | source)
XLA Modules:
  0.0 177.6 jit_solution(7741742582017788787)
XLA Ops:
  0.0 0.8 select_reduce_fusion.1
  0.8 0.7 select_reduce_fusion
  1.5 0.7 select_reduce_fusion.2
  2.2 0.1 copy.22
  2.3 0.1 copy.25
  2.4 0.1 copy.21
  2.5 0.1 copy.24
  2.6 1.8 concatenate.6.blk
  4.4 6.8 %copy.26 = bf16[256,8,2,768]{3,1,2,0:T(8,128)(2,1)} copy(bf16[256,8,2,768]{3,2,1,0:T(2,128)(2,1)} %bitcast.10) | data formatting | bytes 12582912
  11.2 0.0 copy-start
  11.2 0.0 copy-start.1
  11.2 77.9 %layer_0.1 = f32[64,2048]{1,0:T(8,128)} custom-call(bf16[64,2176]{1,0:T(8,128)(2,1)} %concatenate.6.blk, bf16[2048,1536]{1,0:T(8,128)(2,1)} %bitcast.8, bf16[768,2048]{1,0:T(8,128)(2,1)} %bitcast.12), custom_call_target="tpu_custom_call" | custom-call | tf_op jit(solution)/shard_map/layer_0/pallas_call | solution.py:134
  89.2 0.0 copy-done
  89.2 1.2 fusion
  90.4 0.0 copy-done.1
  90.4 0.1 fusion.2
  90.5 0.8 concatenate.7.blk
  91.4 6.8 %copy.27 = bf16[256,8,2,768]{3,1,2,0:T(8,128)(2,1)} copy(bf16[256,8,2,768]{3,2,1,0:T(2,128)(2,1)} %bitcast.11) | data formatting | bytes 12582912
  98.2 77.6 %layer_1.1 = f32[64,2048]{1,0:T(8,128)} custom-call(bf16[64,2176]{1,0:T(8,128)(2,1)} %concatenate.7.blk, bf16[2048,1536]{1,0:T(8,128)(2,1)} %bitcast.9, bf16[768,2048]{1,0:T(8,128)(2,1)} %bitcast.13), custom_call_target="tpu_custom_call" | custom-call | tf_op jit(solution)/shard_map/layer_1/pallas_call | solution.py:134
  175.8 1.8 %fusion.3 = bf16[64,2048]{1,0:T(8,128)(2,1)} fusion(f32[64,2048]{1,0:T(8,128)} %layer_1.1, bf16[64,2048]{1,0:T(8,128)(2,1)S(1)} %get-tuple-element.6), kind=kLoop, calls=%fused_computation.6 | loop fusion | flops 393216 | bytes 1048576 | tf_op jit(solution)/shard_map/convert_element_type | solution.py:187
  (6 shorter events, 0.0 us)
Async XLA Ops:
  11.2 77.9 %copy-start = (bf16[64,2048]{1,0:T(8,128)(2,1)S(1)}, bf16[64,2048]{1,0:T(8,128)(2,1)}, u32[]{:S(2)}) copy-start(bf16[64,2048]{1,0:T(8,128)(2,1)} %param.11) | copy-start | bytes 786436
  11.2 79.2 %copy-start.1 = (f32[2048]{0:T(1024)S(1)}, f32[2048]{0:T(1024)}, u32[]{:S(2)}) copy-start(f32[2048]{0:T(1024)} %param.16) | copy-start | bytes 24580

commit v3 on v2

--- a/solution.py
+++ b/solution.py
@@ -24,7 +24,9 @@
     c_peer = {"dp": d + 1 - 2 * (d % 2)}
     half = w_down.shape[0]
     tok = blk.shape[0]
-    order = sorted(range(n), key=lambda k: (min(k, n - k), k))
+    pair = z + 1 - 2 * (z % 2)
+    order = [z, pair, 2 - z // 2, 3 - 3 * (z // 2)]
+    inner = z % 3 != 0
 
     def remote(src, dst, send, recv, to):
         return pltpu.make_async_remote_copy(
@@ -50,57 +52,67 @@
         sends.append(copy)
         return copy
 
-    z_copy = {}
-    for k in order[1:]:
-        z_copy[k] = go(remote(blk, rows.at[k, 0], z_send.at[k], z_recv.at[k], {"ep": (z + n - k) % n}))
-    x_copy, c_copy, d_copy = {}, {}, {}
-
-    def spread(k):
-        src = blk if k == 0 else rows.at[k, 0]
-        x_copy[k] = go(remote(src, rows.at[k, 1], x_send.at[k], x_recv.at[k], x_peer))
-        c_copy[k] = go(remote(src, rows.at[k, 2], c_send.at[k], c_recv.at[k], c_peer))
+    up = remote(blk, rows.at[z, 0], z_send.at[0], z_recv.at[z], {"ep": (z + 1) % n})
+    down = remote(blk, rows.at[z, 0], z_send.at[n], z_recv.at[z], {"ep": (z + n - 1) % n})
+    has_up, has_down = z < n - 1, z > 0
+    pl.when(has_up)(up.start)
+    pl.when(has_down)(down.start)
+    x_copy, c_copy, d_copy, passed = {}, {}, {}, {}
+
+    def spread(i):
+        b = order[i]
+        src = blk if i == 0 else rows.at[b, 0]
+        x_copy[i] = go(remote(src, rows.at[b, 1], x_send.at[i], x_recv.at[i], x_peer))
+        if i > 0:
+            to = {"ep": 3 - z if i == 1 else pair}
+            passed[i] = remote(src, rows.at[b, 0], z_send.at[i], z_recv.at[b], to)
+            pl.when(inner)(passed[i].start)
+        c_copy[i] = go(remote(src, rows.at[b, 2], c_send.at[i], c_recv.at[i], c_peer))
 
     spread(0)
-    rows[0, 0] = blk[...]
+    rows[z, 0] = blk[...]
     rc_copy, rx_copy, rz_copy = {}, {}, {}
 
-    def finish(k):
-        rx_copy[k].wait_recv()
+    def to_cross(i):
+        rc_copy[i].wait_recv()
+        cross[i] = (part[i, 1].astype(jnp.float32) + core_in[i, 1].astype(jnp.float32)).astype(cross.dtype)
+        rx_copy[i] = go(remote(cross.at[i], x_in.at[i], rx_send.at[i], rx_recv.at[i], x_peer))
+
+    def finish(i):
+        rx_copy[i].wait_recv()
         total = (
-            part[k, 0].astype(jnp.float32) + core_in[k, 0].astype(jnp.float32) + x_in[k].astype(jnp.float32)
+            part[i, 0].astype(jnp.float32) + core_in[i, 0].astype(jnp.float32) + x_in[i].astype(jnp.float32)
         )
-        if k == 0:
+        if i == 0:
             out[...] = total
         else:
-            line[k] = total.astype(line.dtype)
-            rz_copy[n - k] = go(
-                remote(line.at[k], z_in.at[n - k], rz_send.at[k], rz_recv.at[n - k], {"ep": (z + k) % n})
-            )
-
-    for i, k in enumerate(order):
-        x_copy[k].wait_recv()
-        d_copy[k] = go(remote(rows.at[k, 1], rows.at[k, 3], d_send.at[k], d_recv.at[k], c_peer))
+            line[i] = total.astype(line.dtype)
+            go(remote(line.at[i], z_in.at[z], rz_send.at[i], rz_recv.at[z], {"ep": order[i]}))
+
+    for i, b in enumerate(order):
+        x_copy[i].wait_recv()
+        d_copy[i] = go(remote(rows.at[b, 1], rows.at[b, 3], d_send.at[i], d_recv.at[i], c_peer))
         if i + 1 < n:
             later = order[i + 1]
-            z_copy[later].wait_recv()
-            spread(later)
-        c_copy[k].wait_recv()
-        d_copy[k].wait_recv()
+            remote(blk, rows.at[later, 0], z_send.at[0], z_recv.at[later], {"ep": pair}).wait_recv()
+            spread(i + 1)
+        c_copy[i].wait_recv()
+        d_copy[i].wait_recv()
         if i == 0:
             load_in.wait()
             load_down.wait()
-        gates = rows[k, :, :, width:].reshape(4 * tok, LANES).astype(jnp.float32)
+        gates = rows[b, :, :, width:].reshape(4 * tok, LANES).astype(jnp.float32)
         lane = lax.broadcasted_iota(jnp.int32, (4 * tok, LANES), 1)
         weight = jnp.sum(jnp.where((lane == mine) | (lane == mine + experts), gates, 0.0), axis=1, keepdims=True)
         step = 256 if half % 256 == 0 else LANES
 
         @pl.loop(0, half // step)
         def _(j):
-            x = rows[k, :, :, :width].reshape(4 * tok, width)
+            x = rows[b, :, :, :width].reshape(4 * tok, width)
             at = pl.multiple_of(j * step, step)
             gate = jnp.dot(x, w_in[:, pl.ds(at, step)], preferred_element_type=jnp.float32)
-            up = jnp.dot(x, w_in[:, pl.ds(half + at, step)], preferred_element_type=jnp.float32)
-            hidden[:, pl.ds(at, step)] = (gate / (1.0 + jnp.exp(-gate)) * up).astype(hidden.dtype)
+            up_part = jnp.dot(x, w_in[:, pl.ds(half + at, step)], preferred_element_type=jnp.float32)
+            hidden[:, pl.ds(at, step)] = (gate / (1.0 + jnp.exp(-gate)) * up_part).astype(hidden.dtype)
 
         wide = 256 if width % 256 == 0 else LANES
 
@@ -109,18 +121,24 @@
             at = pl.multiple_of(j * wide, wide)
             y = jnp.dot(hidden[...], w_down[:, pl.ds(at, wide)], preferred_element_type=jnp.float32)
             y = jnp.where(weight == 0.0, 0.0, y * weight)
-            part[k, :, :, pl.ds(at, wide)] = y.astype(part.dtype).reshape(4, tok, wide)
-
-        rc_copy[k] = go(remote(part.at[k, pl.ds(2, 2)], core_in.at[k], rc_send.at[k], rc_recv.at[k], c_peer))
+            part[i, :, :, pl.ds(at, wide)] = y.astype(part.dtype).reshape(4, tok, wide)
+
+        rc_copy[i] = go(remote(part.at[i, pl.ds(2, 2)], core_in.at[i], rc_send.at[i], rc_recv.at[i], c_peer))
         if i > 0:
-            finish(order[i - 1])
-        rc_copy[k].wait_recv()
-        cross[k] = (part[k, 1].astype(jnp.float32) + core_in[k, 1].astype(jnp.float32)).astype(cross.dtype)
-        rx_copy[k] = go(remote(cross.at[k], x_in.at[k], rx_send.at[k], rx_recv.at[k], x_peer))
-    finish(order[-1])
-    for k in order[1:]:
-        rz_copy[k].wait_recv()
-        out[...] += z_in[k].astype(jnp.float32)
+            to_cross(i)
+        if i > 1:
+            finish(i - 1)
+    to_cross(0)
+    finish(n - 1)
+    finish(0)
+    for i in range(1, n):
+        b = order[i]
+        remote(line.at[i], z_in.at[b], rz_send.at[0], rz_recv.at[b], {"ep": b}).wait_recv()
+        out[...] += z_in[b].astype(jnp.float32)
+    pl.when(has_up)(up.wait_send)
+    pl.when(has_down)(down.wait_send)
+    for copy in passed.values():
+        pl.when(inner)(copy.wait_send)
     for copy in sends:
         copy.wait_send()
 
@@ -152,8 +170,9 @@
             pltpu.VMEM((half, width), bf16),
             pltpu.VMEM((4 * tok, half), bf16),
             dma((2,)),
+            dma((n + 1,)),
         ]
-        + [dma((n,))] * 14,
+        + [dma((n,))] * 13,
         compiler_params=pltpu.CompilerParams(
             collective_id=number, has_side_effects=True, vmem_limit_bytes=56 * 1024 * 1024
         ),
@@ -309,5 +328,5 @@
         P(("ep", "dp"), "tp", None),
     )
     out_specs = P(("groups", "ep", "dp", "tp"), None)
-    fused = mesh.shape["tp"] == 1 and mesh.shape["dp"] == 4 and mesh.shape["ep"] <= 4
+    fused = mesh.shape["tp"] == 1 and mesh.shape["dp"] == 4 and mesh.shape["ep"] == 4
     return jax.shard_map(fused_shards if fused else shards, mesh=mesh, in_specs=in_specs, out_specs=out_specs, check_vma=False)

time: 178 us -> 169 us (0.949)
  the two profiles are of different devices: /device:TPU:31 before, /device:TPU:0 now
where the time goes in v3:
time: 169 us
  Pallas kernels  147 us (87%)
  local copies, waits for them, and re-layouts  16.6 us (10%)
  other arithmetic  5.39 us (3%)
    pallas_call x2, Pallas kernels, expert_layer(): pl.pallas_call(functools.partial(layer_kernel, n, experts, width), out_sh...  147 us
    unnamed x6, local copies, waits for them, and re-layouts  13.6 us

profile of v3, /device:TPU:0, one launch (start us, length us, event | category | flops | bytes accessed | tf_op | source)
XLA Modules:
  0.0 168.7 jit_solution(13416676045670740760)
XLA Ops:
  0.0 0.8 select_reduce_fusion.1
  0.8 0.7 select_reduce_fusion
  1.5 0.7 select_reduce_fusion.2
  2.2 0.1 copy.22
  2.3 0.1 copy.25
  2.4 0.1 copy.21
  2.5 0.1 copy.24
  2.6 1.8 %concatenate.6.blk = bf16[64,2176]{1,0:T(8,128)(2,1)} concatenate(bf16[64,2048]{1,0:T(8,128)(2,1)} %param.11, bf16[64,16]{1,0:T(8,128)(2,1)S(1)} %copy.22, bf16[64,16]{1,0:T(8,128)(2,1)S(1)} %subtract_convert_fusion.1, bf16[64,96]{1,0:T(8,128)(2,1)S(1)} %broadcast.21), dimensions={1} | concatenate | bytes 557056 | tf_op jit(solution)/shard_map/concatenate | solution.py:189
  4.4 6.8 %copy.26 = bf16[256,8,2,768]{3,1,2,0:T(8,128)(2,1)} copy(bf16[256,8,2,768]{3,2,1,0:T(2,128)(2,1)} %bitcast.10) | data formatting | bytes 12582912
  11.2 0.0 copy-start
  11.2 0.0 copy-start.1
  11.2 74.6 %layer_0.1 = f32[64,2048]{1,0:T(8,128)} custom-call(bf16[64,2176]{1,0:T(8,128)(2,1)} %concatenate.6.blk, bf16[2048,1536]{1,0:T(8,128)(2,1)} %bitcast.8, bf16[768,2048]{1,0:T(8,128)(2,1)} %bitcast.12), custom_call_target="tpu_custom_call" | custom-call | tf_op jit(solution)/shard_map/layer_0/pallas_call | solution.py:152
  85.8 0.0 copy-done
  85.8 1.2 fusion
  87.0 0.0 copy-done.1
  87.0 0.1 fusion.2
  87.2 0.8 concatenate.7.blk
  88.0 6.8 %copy.27 = bf16[256,8,2,768]{3,1,2,0:T(8,128)(2,1)} copy(bf16[256,8,2,768]{3,2,1,0:T(2,128)(2,1)} %bitcast.11) | data formatting | bytes 12582912
  94.8 72.1 %layer_1.1 = f32[64,2048]{1,0:T(8,128)} custom-call(bf16[64,2176]{1,0:T(8,128)(2,1)} %concatenate.7.blk, bf16[2048,1536]{1,0:T(8,128)(2,1)} %bitcast.9, bf16[768,2048]{1,0:T(8,128)(2,1)} %bitcast.13), custom_call_target="tpu_custom_call" | custom-call | tf_op jit(solution)/shard_map/layer_1/pallas_call | solution.py:152
  166.9 1.8 %fusion.3 = bf16[64,2048]{1,0:T(8,128)(2,1)} fusion(f32[64,2048]{1,0:T(8,128)} %layer_1.1, bf16[64,2048]{1,0:T(8,128)(2,1)S(1)} %get-tuple-element.6), kind=kLoop, calls=%fused_computation.6 | loop fusion | flops 393216 | bytes 1048576 | tf_op jit(solution)/shard_map/convert_element_type | solution.py:206
  (6 shorter events, 0.0 us)
Async XLA Ops:
  11.2 74.6 %copy-start = (bf16[64,2048]{1,0:T(8,128)(2,1)S(1)}, bf16[64,2048]{1,0:T(8,128)(2,1)}, u32[]{:S(2)}) copy-start(bf16[64,2048]{1,0:T(8,128)(2,1)} %param.11) | copy-start | bytes 786436
  11.2 75.8 %copy-start.1 = (f32[2048]{0:T(1024)S(1)}, f32[2048]{0:T(1024)}, u32[]{:S(2)}) copy-start(f32[2048]{0:T(1024)} %param.16) | copy-start | bytes 24580

commit v4 on v3

--- a/solution.py
+++ b/solution.py
@@ -13,7 +13,7 @@
 
 def layer_kernel(
     n, experts, width, blk, w_in_hbm, w_down_hbm, out,
-    rows, part, core_in, cross, x_in, line, z_in, w_in, w_down, hidden,
+    rows, part, core_in, cross, x_in, line, z_in, raw, w_in, w_down, hidden,
     w_sem, z_send, z_recv, x_send, x_recv, c_send, c_recv, d_send, d_recv,
     rc_send, rc_recv, rx_send, rx_recv, rz_send, rz_recv,
 ):
@@ -33,7 +33,7 @@
             src_ref=src, dst_ref=dst, send_sem=send, recv_sem=recv, device_id=to, device_id_type=MESH
         )
 
-    load_in = pltpu.make_async_copy(w_in_hbm, w_in, w_sem.at[0])
+    load_in = pltpu.make_async_copy(w_in_hbm, raw, w_sem.at[0])
     load_down = pltpu.make_async_copy(w_down_hbm, w_down, w_sem.at[1])
     load_in.start()
     load_down.start()
@@ -52,55 +52,90 @@
         sends.append(copy)
         return copy
 
-    up = remote(blk, rows.at[z, 0], z_send.at[0], z_recv.at[z], {"ep": (z + 1) % n})
-    down = remote(blk, rows.at[z, 0], z_send.at[n], z_recv.at[z], {"ep": (z + n - 1) % n})
+    size = tok // 2
+    halves = [pl.ds(h * size, size) for h in range(2)]
     has_up, has_down = z < n - 1, z > 0
-    pl.when(has_up)(up.start)
-    pl.when(has_down)(down.start)
-    x_copy, c_copy, d_copy, passed = {}, {}, {}, {}
-
-    def spread(i):
+    outer = jnp.logical_not(inner)
+    ups, downs = [], []
+    for h, at in enumerate(halves):
+        own = blk.at[at]
+        ups.append(remote(own, rows.at[z, 0, at], z_send.at[0, h], z_recv.at[z, h], {"ep": (z + 1) % n}))
+        downs.append(remote(own, rows.at[z, 0, at], z_send.at[n, h], z_recv.at[z, h], {"ep": (z + n - 1) % n}))
+    x_copy, c_copy, d_copy = {}, {}, {}
+    for i, b in enumerate(order):
+        src = blk if i == 0 else rows.at[b, 0]
+        for h, at in enumerate(halves):
+            x_copy[i, h] = remote(src.at[at], rows.at[b, 1, at], x_send.at[i, h], x_recv.at[i, h], x_peer)
+        c_copy[i] = remote(src, rows.at[b, 2], c_send.at[i], c_recv.at[i], c_peer)
+        d_copy[i] = remote(rows.at[b, 1], rows.at[b, 3], d_send.at[i], d_recv.at[i], c_peer)
+        sends += [x_copy[i, 0], x_copy[i, 1], c_copy[i], d_copy[i]]
+
+    def arrive(i, relay):
         b = order[i]
-        src = blk if i == 0 else rows.at[b, 0]
-        x_copy[i] = go(remote(src, rows.at[b, 1], x_send.at[i], x_recv.at[i], x_peer))
-        if i > 0:
-            to = {"ep": 3 - z if i == 1 else pair}
-            passed[i] = remote(src, rows.at[b, 0], z_send.at[i], z_recv.at[b], to)
-            pl.when(inner)(passed[i].start)
-        c_copy[i] = go(remote(src, rows.at[b, 2], c_send.at[i], c_recv.at[i], c_peer))
-
-    spread(0)
+        to = {"ep": 3 - z if i == 1 else pair}
+        for h, at in enumerate(halves):
+            move = remote(rows.at[b, 0, at], rows.at[b, 0, at], z_send.at[i, h], z_recv.at[b, h], to)
+            move.wait_recv()
+            if relay:
+                pl.when(inner)(move.start)
+            x_copy[i, h].start()
+        c_copy[i].start()
+
+    for h in range(2):
+        pl.when(has_up)(ups[h].start)
+        pl.when(has_down)(downs[h].start)
+        x_copy[0, h].start()
+    c_copy[0].start()
     rows[z, 0] = blk[...]
-    rc_copy, rx_copy, rz_copy = {}, {}, {}
+    load_in.wait()
+    group = 128
+
+    @pl.loop(0, w_in.shape[0] // group)
+    def _(j):
+        at = pl.ds(pl.multiple_of(j * group, group), group)
+        w_in[at, :half] = raw[at, 0, :]
+        w_in[at, half:] = raw[at, 1, :]
+
+    load_down.wait()
+    rc_copy, rx_copy = {}, {}
 
     def to_cross(i):
         rc_copy[i].wait_recv()
-        cross[i] = (part[i, 1].astype(jnp.float32) + core_in[i, 1].astype(jnp.float32)).astype(cross.dtype)
-        rx_copy[i] = go(remote(cross.at[i], x_in.at[i], rx_send.at[i], rx_recv.at[i], x_peer))
+        for h, at in enumerate(halves):
+            value = part[i, 1, at].astype(jnp.float32) + core_in[i, 1, at].astype(jnp.float32)
+            cross[i, at] = value.astype(cross.dtype)
+            rx_copy[i, h] = go(
+                remote(cross.at[i, at], x_in.at[i, at], rx_send.at[i, h], rx_recv.at[i, h], x_peer)
+            )
 
     def finish(i):
-        rx_copy[i].wait_recv()
-        total = (
-            part[i, 0].astype(jnp.float32) + core_in[i, 0].astype(jnp.float32) + x_in[i].astype(jnp.float32)
-        )
+        for h, at in enumerate(halves):
+            rx_copy[i, h].wait_recv()
+            total = (
+                part[i, 0, at].astype(jnp.float32)
+                + core_in[i, 0, at].astype(jnp.float32)
+                + x_in[i, at].astype(jnp.float32)
+            )
+            if i == 0:
+                out[at] = total
+            else:
+                line[i, at] = total.astype(line.dtype)
+                go(remote(line.at[i, at], z_in.at[z, at], rz_send.at[i, h], rz_recv.at[z, h], {"ep": order[i]}))
+
+    for i, b in enumerate(order):
         if i == 0:
-            out[...] = total
-        else:
-            line[i] = total.astype(line.dtype)
-            go(remote(line.at[i], z_in.at[z], rz_send.at[i], rz_recv.at[z], {"ep": order[i]}))
-
-    for i, b in enumerate(order):
-        x_copy[i].wait_recv()
-        d_copy[i] = go(remote(rows.at[b, 1], rows.at[b, 3], d_send.at[i], d_recv.at[i], c_peer))
-        if i + 1 < n:
-            later = order[i + 1]
-            remote(blk, rows.at[later, 0], z_send.at[0], z_recv.at[later], {"ep": pair}).wait_recv()
-            spread(i + 1)
+            arrive(1, True)
+            pl.when(inner)(functools.partial(arrive, 2, True))
+        elif i == 1:
+            pl.when(outer)(functools.partial(arrive, 2, False))
+            pl.when(inner)(functools.partial(arrive, 3, True))
+        elif i == 2:
+            pl.when(outer)(functools.partial(arrive, 3, False))
+        for h in range(2):
+            x_copy[i, h].wait_recv()
+        d_copy[i].start()
         c_copy[i].wait_recv()
         d_copy[i].wait_recv()
-        if i == 0:
-            load_in.wait()
-            load_down.wait()
         gates = rows[b, :, :, width:].reshape(4 * tok, LANES).astype(jnp.float32)
         lane = lax.broadcasted_iota(jnp.int32, (4 * tok, LANES), 1)
         weight = jnp.sum(jnp.where((lane == mine) | (lane == mine + experts), gates, 0.0), axis=1, keepdims=True)
@@ -126,19 +161,24 @@
         rc_copy[i] = go(remote(part.at[i, pl.ds(2, 2)], core_in.at[i], rc_send.at[i], rc_recv.at[i], c_peer))
         if i > 0:
             to_cross(i)
+        if i == n - 1:
+            to_cross(0)
         if i > 1:
             finish(i - 1)
-    to_cross(0)
     finish(n - 1)
     finish(0)
     for i in range(1, n):
         b = order[i]
-        remote(line.at[i], z_in.at[b], rz_send.at[0], rz_recv.at[b], {"ep": b}).wait_recv()
-        out[...] += z_in[b].astype(jnp.float32)
-    pl.when(has_up)(up.wait_send)
-    pl.when(has_down)(down.wait_send)
-    for copy in passed.values():
-        pl.when(inner)(copy.wait_send)
+        for h, at in enumerate(halves):
+            remote(line.at[i, at], z_in.at[b, at], rz_send.at[0, h], rz_recv.at[b, h], {"ep": b}).wait_recv()
+            out[at] += z_in[b, at].astype(jnp.float32)
+    for h in range(2):
+        pl.when(has_up)(ups[h].wait_send)
+        pl.when(has_down)(downs[h].wait_send)
+    for i in range(1, n):
+        for h, at in enumerate(halves):
+            spot = rows.at[order[i], 0, at]
+            pl.when(inner)(remote(spot, spot, z_send.at[i, h], z_recv.at[0, h], {"ep": pair}).wait_send)
     for copy in sends:
         copy.wait_send()
 
@@ -166,18 +206,23 @@
             pltpu.VMEM((n, tok, width), bf16),
             pltpu.VMEM((n, tok, width), bf16),
             pltpu.VMEM((n, tok, width), bf16),
+            pltpu.VMEM((width, 2, half), bf16),
             pltpu.VMEM((width, 2 * half), bf16),
             pltpu.VMEM((half, width), bf16),
             pltpu.VMEM((4 * tok, half), bf16),
             dma((2,)),
-            dma((n + 1,)),
+            dma((n + 1, 2)),
+            dma((n, 2)),
+            dma((n, 2)),
+            dma((n, 2)),
         ]
-        + [dma((n,))] * 13,
+        + [dma((n,))] * 6
+        + [dma((n, 2))] * 4,
         compiler_params=pltpu.CompilerParams(
             collective_id=number, has_side_effects=True, vmem_limit_bytes=56 * 1024 * 1024
         ),
         name=f"layer_{number}",
-    )(block, w_in.reshape(width, 2 * half), w_down.reshape(half, width))
+    )(block, w_in.reshape(width, 2, half), w_down.reshape(half, width))
 
 
 def with_gates(rows_in, targets, gate_values, experts):
@@ -328,5 +373,9 @@
         P(("ep", "dp"), "tp", None),
     )
     out_specs = P(("groups", "ep", "dp", "tp"), None)
-    fused = mesh.shape["tp"] == 1 and mesh.shape["dp"] == 4 and mesh.shape["ep"] == 4
-    return jax.shard_map(fused_shards if fused else shards, mesh=mesh, in_specs=in_specs, out_specs=out_specs, check_vma=False)
+    ready = mesh.shape["tp"] == 1 and mesh.shape["dp"] == 4 and mesh.shape["ep"] == 4
+
+    def body(*arrays):
+        return (fused_shards if ready and arrays[0].shape[0] % 32 == 0 else shards)(*arrays)
+
+    return jax.shard_map(body, mesh=mesh, in_specs=in_specs, out_specs=out_specs, check_vma=False)

time: 169 us -> 163 us (0.964)
  local copies, waits for them, and re-layouts: 16.6 us -> 2.92 us
  Pallas kernels: 147 us -> 154 us
    unnamed x6 -> x4, local copies, waits for them, and re-layouts: 13.6 us -> 0.01 us
    pallas_call x2, Pallas kernels: 147 us -> 154 us  [expert_layer(): pl.pallas_call(functools.partial(layer_kernel, n, experts, width), out_sh...]
where the time goes in v4:
time: 163 us
  Pallas kernels  154 us (94%)
  other arithmetic  5.44 us (3%)
  local copies, waits for them, and re-layouts  2.92 us (2%)
    pallas_call x2, Pallas kernels, expert_layer(): pl.pallas_call(functools.partial(layer_kernel, n, experts, width), out_sh...  154 us

profile of v4, /device:TPU:0, one launch (start us, length us, event | category | flops | bytes accessed | tf_op | source)
XLA Modules:
  0.0 162.7 jit_solution(1807137364600311217)
XLA Ops:
  0.0 0.0 copy-start
  0.0 0.0 copy-start.1
  0.0 0.8 select_reduce_fusion.1
  0.8 0.7 select_reduce_fusion
  1.6 0.7 select_reduce_fusion.2
  2.3 0.1 copy.22
  2.4 0.1 copy.25
  2.5 0.1 copy.21
  2.6 0.1 copy.24
  2.7 1.7 %concatenate.6.blk = bf16[64,2176]{1,0:T(8,128)(2,1)} concatenate(bf16[64,2048]{1,0:T(8,128)(2,1)} %param.11, bf16[64,16]{1,0:T(8,128)(2,1)S(1)} %copy.22, bf16[64,16]{1,0:T(8,128)(2,1)S(1)} %subtract_convert_fusion.1, bf16[64,96]{1,0:T(8,128)(2,1)S(1)} %broadcast.21), dimensions={1} | concatenate | bytes 557056 | tf_op jit(solution)/shard_map/concatenate | solution.py:234
  4.4 79.9 %layer_0.1 = f32[64,2048]{1,0:T(8,128)} custom-call(bf16[64,2176]{1,0:T(8,128)(2,1)} %concatenate.6.blk, bf16[2048,2,768]{2,1,0:T(2,128)(2,1)} %bitcast.4, bf16[768,2048]{1,0:T(8,128)(2,1)} %bitcast.6), custom_call_target="tpu_custom_call" | custom-call | tf_op jit(solution)/shard_map/layer_0/pallas_call | solution.py:192
  84.3 0.0 copy-done
  84.3 1.2 fusion
  85.6 0.0 copy-done.1
  85.6 0.1 fusion.2
  85.7 0.8 concatenate.7.blk
  86.5 74.4 %layer_1.1 = f32[64,2048]{1,0:T(8,128)} custom-call(bf16[64,2176]{1,0:T(8,128)(2,1)} %concatenate.7.blk, bf16[2048,2,768]{2,1,0:T(2,128)(2,1)} %bitcast.5, bf16[768,2048]{1,0:T(8,128)(2,1)} %bitcast.7), custom_call_target="tpu_custom_call" | custom-call | tf_op jit(solution)/shard_map/layer_1/pallas_call | solution.py:192
  161.0 1.8 %fusion.3 = bf16[64,2048]{1,0:T(8,128)(2,1)} fusion(f32[64,2048]{1,0:T(8,128)} %layer_1.1, bf16[64,2048]{1,0:T(8,128)(2,1)S(1)} %get-tuple-element.6), kind=kLoop, calls=%fused_computation.6 | loop fusion | flops 393216 | bytes 1048576 | tf_op jit(solution)/shard_map/convert_element_type | solution.py:251
  (6 shorter events, 0.0 us)
Async XLA Ops:
  0.0 84.3 %copy-start = (bf16[64,2048]{1,0:T(8,128)(2,1)S(1)}, bf16[64,2048]{1,0:T(8,128)(2,1)}, u32[]{:S(2)}) copy-start(bf16[64,2048]{1,0:T(8,128)(2,1)} %param.11) | copy-start | bytes 786436
  0.0 85.6 %copy-start.1 = (f32[2048]{0:T(1024)S(1)}, f32[2048]{0:T(1024)}, u32[]{:S(2)}) copy-start(f32[2048]{0:T(1024)} %param.16) | copy-start | bytes 24580

commit v5 on v4

--- a/solution.py
+++ b/solution.py
@@ -87,16 +87,6 @@
         x_copy[0, h].start()
     c_copy[0].start()
     rows[z, 0] = blk[...]
-    load_in.wait()
-    group = 128
-
-    @pl.loop(0, w_in.shape[0] // group)
-    def _(j):
-        at = pl.ds(pl.multiple_of(j * group, group), group)
-        w_in[at, :half] = raw[at, 0, :]
-        w_in[at, half:] = raw[at, 1, :]
-
-    load_down.wait()
     rc_copy, rx_copy = {}, {}
 
     def to_cross(i):
@@ -134,6 +124,16 @@
         for h in range(2):
             x_copy[i, h].wait_recv()
         d_copy[i].start()
+        if i == 0:
+            load_in.wait()
+            group = 128
+
+            @pl.loop(0, w_in.shape[0] // group)
+            def _(j):
+                at = pl.ds(pl.multiple_of(j * group, group), group)
+                w_in[at] = raw[at].reshape(group, 2 * half)
+
+            load_down.wait()
         c_copy[i].wait_recv()
         d_copy[i].wait_recv()
         gates = rows[b, :, :, width:].reshape(4 * tok, LANES).astype(jnp.float32)
@@ -149,14 +149,9 @@
             up_part = jnp.dot(x, w_in[:, pl.ds(half + at, step)], preferred_element_type=jnp.float32)
             hidden[:, pl.ds(at, step)] = (gate / (1.0 + jnp.exp(-gate)) * up_part).astype(hidden.dtype)
 
-        wide = 256 if width % 256 == 0 else LANES
-
-        @pl.loop(0, width // wide)
-        def _(j):
-            at = pl.multiple_of(j * wide, wide)
-            y = jnp.dot(hidden[...], w_down[:, pl.ds(at, wide)], preferred_element_type=jnp.float32)
-            y = jnp.where(weight == 0.0, 0.0, y * weight)
-            part[i, :, :, pl.ds(at, wide)] = y.astype(part.dtype).reshape(4, tok, wide)
+        y = jnp.dot(hidden[...], w_down[...], preferred_element_type=jnp.float32)
+        y = jnp.where(weight == 0.0, 0.0, y * weight)
+        part[i] = y.astype(part.dtype).reshape(4, tok, width)
 
         rc_copy[i] = go(remote(part.at[i, pl.ds(2, 2)], core_in.at[i], rc_send.at[i], rc_recv.at[i], c_peer))
         if i > 0:

time: 163 us -> 142 us (0.87)
  Pallas kernels: 154 us -> 134 us
    pallas_call x2, Pallas kernels: 154 us -> 134 us  [expert_layer(): pl.pallas_call(functools.partial(layer_kernel, n, experts, width), out_sh...]
where the time goes in v5:
time: 142 us
  Pallas kernels  134 us (94%)
  other arithmetic  5.44 us (4%)
  local copies, waits for them, and re-layouts  2.92 us (2%)
    pallas_call x2, Pallas kernels, expert_layer(): pl.pallas_call(functools.partial(layer_kernel, n, experts, width), out_sh...  134 us

profile of v5, /device:TPU:0, one launch (start us, length us, event | category | flops | bytes accessed | tf_op | source)
XLA Modules:
  0.0 142.0 jit_solution(4362707304191840145)
XLA Ops:
  0.0 0.0 copy-start
  0.0 0.0 copy-start.1
  0.0 0.8 select_reduce_fusion.1
  0.8 0.7 select_reduce_fusion
  1.6 0.7 select_reduce_fusion.2
  2.3 0.1 copy.22
  2.4 0.1 copy.25
  2.5 0.1 copy.21
  2.6 0.1 copy.24
  2.7 1.7 %concatenate.6.blk = bf16[64,2176]{1,0:T(8,128)(2,1)} concatenate(bf16[64,2048]{1,0:T(8,128)(2,1)} %param.11, bf16[64,16]{1,0:T(8,128)(2,1)S(1)} %copy.22, bf16[64,16]{1,0:T(8,128)(2,1)S(1)} %subtract_convert_fusion.1, bf16[64,96]{1,0:T(8,128)(2,1)S(1)} %broadcast.21), dimensions={1} | concatenate | bytes 557056 | tf_op jit(solution)/shard_map/concatenate | solution.py:229
  4.4 69.5 %layer_0.1 = f32[64,2048]{1,0:T(8,128)} custom-call(bf16[64,2176]{1,0:T(8,128)(2,1)} %concatenate.6.blk, bf16[2048,2,768]{2,1,0:T(2,128)(2,1)} %bitcast.4, bf16[768,2048]{1,0:T(8,128)(2,1)} %bitcast.6), custom_call_target="tpu_custom_call" | custom-call | tf_op jit(solution)/shard_map/layer_0/pallas_call | solution.py:187
  74.0 0.0 copy-done
  74.0 1.2 fusion
  75.2 0.0 copy-done.1
  75.2 0.1 fusion.2
  75.4 0.8 concatenate.7.blk
  76.2 64.1 %layer_1.1 = f32[64,2048]{1,0:T(8,128)} custom-call(bf16[64,2176]{1,0:T(8,128)(2,1)} %concatenate.7.blk, bf16[2048,2,768]{2,1,0:T(2,128)(2,1)} %bitcast.5, bf16[768,2048]{1,0:T(8,128)(2,1)} %bitcast.7), custom_call_target="tpu_custom_call" | custom-call | tf_op jit(solution)/shard_map/layer_1/pallas_call | solution.py:187
  140.2 1.8 %fusion.3 = bf16[64,2048]{1,0:T(8,128)(2,1)} fusion(f32[64,2048]{1,0:T(8,128)} %layer_1.1, bf16[64,2048]{1,0:T(8,128)(2,1)S(1)} %get-tuple-element.6), kind=kLoop, calls=%fused_computation.6 | loop fusion | flops 393216 | bytes 1048576 | tf_op jit(solution)/shard_map/convert_element_type | solution.py:246
  (6 shorter events, 0.0 us)
Async XLA Ops:
  0.0 74.0 %copy-start = (bf16[64,2048]{1,0:T(8,128)(2,1)S(1)}, bf16[64,2048]{1,0:T(8,128)(2,1)}, u32[]{:S(2)}) copy-start(bf16[64,2048]{1,0:T(8,128)(2,1)} %param.11) | copy-start | bytes 786436
  0.0 75.2 %copy-start.1 = (f32[2048]{0:T(1024)S(1)}, f32[2048]{0:T(1024)}, u32[]{:S(2)}) copy-start(f32[2048]{0:T(1024)} %param.16) | copy-start | bytes 24580
